TPU v7x, 32 devices: a whole 2x2x4 slice. The times are simulated.
32 devices in a mesh: group: 2 (over y), seq: 4 (over z), tensor: 4 (over x, core).
Axes of the slice: x: 2, y: 2, z: 4, core: 2. Of those that a mesh axis runs over, the one named last changes fastest.
Arguments:
- query: bfloat16 [16, 7168], P(('group', 'seq'), 'tensor'), parts along dimension 0, may hold values from -5 to 5
- key_cache: bfloat16 [32, 256, 7168], P(('group', 'seq'), None, 'tensor'), parts along dimension 0, may hold values from -5 to 5
- value_cache: bfloat16 [32, 256, 7168], P(('group', 'seq'), None, 'tensor'), parts along dimension 0, may hold values from -6 to 6
- alibi_slopes: float32 [56], P('tensor'), may hold values from 0 to 1, as said below
- block_seq: int32 [32], P(('group', 'seq')), parts along dimension 0, may hold values from 0 to 7, as said below
- block_pos: int32 [32], P(('group', 'seq')), parts along dimension 0, may hold values from 0 to 2, as said below
- lengths: int32 [16], P('group'), parts along dimension 0, may hold values from 1 to 768, as said below
- out_weight: bfloat16 [7168, 14336], P('tensor', 'seq'), may hold values from -0.5 to 0.5
Outputs:
- mixed: bfloat16 [16, 14336], P(('group', 'tensor'), 'seq'), parts along dimension 0
There are 2 independent parts, one for each index of `group`. A program takes and returns all parts, laid end to end along the dimension named above; an argument that names none is the same for every part. Nothing has to cross between parts.
Inputs may be any that keep to these rules, and one draw needn't show every extreme that they name: `block_seq`: every sequence owns at least one block and at most 3; the blocks of sequence s have block_pos 0 to n_s - 1, each once. block_pos of a block is below the number of blocks its sequence owns. `lengths`: A sequence that owns n blocks has a length above 256 * (n - 1) and at most 256 * n. `alibi_slopes`: positive slopes.
All inputs are finite; a program needn't handle non-finite values.
Results may differ from a plain program's by a relative error of at most 0.0054.
Values may be sent and summed in bfloat16 or wider, within the bound.
No kernel may reach another device: no remote copies, remote signals or barrier semaphores. Data moves between devices by JAX's collectives and lax.ppermute only.
A program may use at most 64 MiB of HBM per device.

v0:
```python
import math
import jax
import jax.numpy as jnp
from jax import lax
from jax.sharding import PartitionSpec as P


def local(query, key_cache, value_cache, alibi_slopes, block_seq, block_pos, lengths, out_weight):
    heads = alibi_slopes.shape[0]
    features = query.shape[1]
    head_size = features // heads
    blocks_here = key_cache.shape[0]
    block_len = key_cache.shape[1]
    seq_count = lengths.shape[0]
    scale = 1.0 / math.sqrt(head_size)
    whole_query = lax.all_gather(query, "seq", axis=0, tiled=True)
    query_rows = jnp.take(whole_query, block_seq, axis=0).reshape(blocks_here, heads, head_size)
    keys = key_cache.reshape(blocks_here, block_len, heads, head_size)
    values = value_cache.reshape(blocks_here, block_len, heads, head_size)
    scores = (
        jnp.einsum("bthd,bhd->bht", keys, query_rows, preferred_element_type=jnp.float32) * scale
    )
    owner_length = lengths[block_seq]
    placed = block_pos[:, None] * block_len + jnp.arange(block_len, dtype=jnp.int32)[None, :]
    live = (placed < owner_length[:, None])[:, None, :]
    distance = (owner_length[:, None] - 1 - placed).astype(jnp.float32)
    scores = scores - alibi_slopes[None, :, None] * distance[:, None, :]
    scores = jnp.where(live, scores, -1e30)
    block_top = jnp.max(scores, axis=2)
    weights = jnp.where(live, jnp.exp(scores - block_top[:, :, None]), 0.0)
    block_total = jnp.sum(weights, axis=2)
    block_acc = jnp.einsum(
        "bht,bthd->bhd", weights.astype(jnp.bfloat16), values, preferred_element_type=jnp.float32
    )
    seq_ids = jnp.arange(seq_count, dtype=jnp.int32)
    owned = (block_seq[None, :] == seq_ids[:, None])[:, :, None]
    local_top = jnp.max(jnp.where(owned, block_top[None], -1e30), axis=1)
    factor = jnp.where(owned, jnp.exp(block_top[None] - local_top[:, None, :]), 0.0)
    local_total = jnp.sum(factor * block_total[None], axis=1)
    local_acc = jnp.einsum("sbh,bhd->shd", factor, block_acc, precision=lax.Precision.HIGHEST)
    tops, totals, accs = (
        lax.all_to_all(local_top[None], "seq", split_axis=1, concat_axis=0, tiled=True),
        lax.all_to_all(local_total[None], "seq", split_axis=1, concat_axis=0, tiled=True),
        lax.all_to_all(local_acc[None], "seq", split_axis=1, concat_axis=0, tiled=True),
    )
    best = jnp.max(tops, axis=0)
    scaling = jnp.exp(tops - best[None])
    home_total = jnp.sum(totals * scaling, axis=0)
    home_acc = jnp.sum(accs * scaling[..., None], axis=0)
    mine = (
        (home_acc / home_total[:, :, None])
        .astype(jnp.bfloat16)
        .reshape(home_acc.shape[0], features)
    )
    attention = lax.all_gather(mine, "seq", axis=0, tiled=True)
    mixed = lax.psum_scatter(
        jnp.dot(attention, out_weight, preferred_element_type=jnp.float32),
        "tensor",
        scatter_dimension=0,
        tiled=True,
    )
    return mixed.astype(jnp.bfloat16)


def solution(mesh):
    placed = (
        P(("group", "seq"), "tensor"),
        P(("group", "seq"), None, "tensor"),
        P(("group", "seq"), None, "tensor"),
        P("tensor"),
        P(("group", "seq")),
        P(("group", "seq")),
        P("group"),
        P("tensor", "seq"),
    )
    return jax.shard_map(
        local, mesh=mesh, in_specs=placed, out_specs=P(("group", "tensor"), "seq"), check_vma=False
    )
```

profile of v0, /device:TPU:0, one launch (start us, length us, event | category | flops | bytes accessed | tf_op | source)
XLA Modules:
  0.0 95.4 jit_solution(14486349411866468453)
XLA Ops:
  0.0 0.0 copy-start
  0.0 0.7 compare_select_fusion
  0.7 0.7 compare_and_fusion
  1.3 0.7 iota_compare_fusion
  2.1 0.0 copy-done
  2.1 0.6 gather_fusion
  2.7 0.7 broadcast_add_fusion
  3.4 0.1 fusion.16
  3.5 0.1 subtract_convert_fusion
  3.5 15.1 %all-gather = bf16[4,2,1792]{2,1,0:T(2,128)(2,1)S(1)} all-gather(bf16[1,2,1792]{2,1,0:T(2,128)(2,1)} %bitcast.41), channel_id=1, replica_groups=mesh['group'=2,'seq'=4,'tensor'=4] {'seq'}, dimensions={0}, use_global_device_ids=true | all-gather | bytes 35840 | tf_op jit(solution)/shard_map/all_gather | solution.py:16
  18.6 0.6 gather_fusion.1
  19.2 6.0 %copy.49 = bf16[4,256,1792]{1,2,0:T(8,128)(2,1)} copy(bf16[4,256,1792]{2,1,0:T(8,128)(2,1)} %param.9) | data formatting | bytes 7340032 | tf_op args[1]
  25.2 0.0 copy-start.1
  25.2 0.1 select_bitcast_fusion
  25.3 2.6 %fusion.9 = f32[4,14,1,256]{3,2,1,0:T(1,128)S(1)} fusion(bf16[4,256,14,128]{1,3,2,0:T(8,128)(2,1)} %bitcast.33, bf16[4,14,128,1]{2,1,0,3:T(8,128)(2,1)S(1)} %select_bitcast_fusion), kind=kOutput, calls=%fused_computation.16 | convolution fusion | flops 3670016 | bytes 3741696 | tf_op jit(solution)/shard_map/bthd,bhd->bht/dot_general | solution.py:21
  27.9 0.0 copy-done.1
  27.9 0.2 fusion.18
  28.0 0.1 select_reduce_fusion
  28.1 0.7 copy.54
  28.8 4.7 %all-to-all-start.1 = ((f32[1,8,14]{2,0,1:T(1,128)}), f32[1,8,14]{2,0,1:T(1,128)S(1)}, u32[]{:S(2)}, u32[]{:S(2)}) async-start(f32[1,8,14]{2,0,1:T(1,128)} %copy.54), calls=%async_computation.1 | async-start | bytes 8192 | tf_op jit(solution)/shard_map/all_to_all | solution.py:42
  33.6 0.2 fusion.4
  33.7 0.1 multiply_reduce_fusion.1
  33.8 6.0 %copy.50 = bf16[4,256,1792]{1,2,0:T(8,128)(2,1)} copy(bf16[4,256,1792]{2,1,0:T(8,128)(2,1)} %param.10) | data formatting | bytes 7340032 | tf_op args[2]
  39.8 0.0 copy-start.2
  39.8 3.1 %fusion.2 = f32[4,14,1,128]{3,2,1,0:T(1,128)S(1)} fusion(bf16[4,256,14,128]{1,3,2,0:T(8,128)(2,1)} %bitcast.34, bf16[4,14,256,1]{2,0,1,3:T(4,128)(2,1)S(1)} %get-tuple-element.10), kind=kOutput, calls=%fused_computation.6 | convolution fusion | flops 3670016 | bytes 3727360 | tf_op jit(solution)/shard_map/bht,bthd->bhd/dot_general | solution.py:32
  42.9 0.4 convolution_bitcast_fusion
  43.3 0.7 copy.57
  44.0 0.0 all-to-all-done.1
  44.0 5.1 %all-to-all-start.2 = ((f32[1,8,14]{2,0,1:T(1,128)}), f32[1,8,14]{2,0,1:T(1,128)S(1)}, u32[]{:S(2)}, u32[]{:S(2)}) async-start(f32[1,8,14]{2,0,1:T(1,128)} %copy.57), calls=%async_computation.2 | async-start | bytes 8192 | tf_op jit(solution)/shard_map/all_to_all | solution.py:43
  49.1 0.7 copy.51
  49.7 0.0 copy-done.2
  49.7 0.6 dynamic-slice
  51.0 3.7 %all-to-all-done.2 = f32[1,8,14]{2,0,1:T(1,128)S(1)} async-done(((f32[1,8,14]{2,0,1:T(1,128)}), f32[1,8,14]{2,0,1:T(1,128)S(1)}, u32[]{:S(2)}, u32[]{:S(2)}) %all-to-all-start.2) | async-done | bytes 480 | tf_op jit(solution)/shard_map/all_to_all | solution.py:43
  54.6 3.3 %all-to-all-start = ((f32[1,8,14,128]{3,0,2,1:T(1,128)}), f32[1,8,14,128]{3,0,2,1:T(1,128)S(1)}, u32[]{:S(2)}, u32[]{:S(2)}) async-start(f32[1,8,14,128]{3,0,2,1:T(1,128)} %copy.51), calls=%async_computation | async-start | bytes 114688 | tf_op jit(solution)/shard_map/all_to_all | solution.py:44
  58.0 0.1 copy.55
  58.1 0.1 copy.58
  58.2 5.5 %all-to-all-done = f32[1,8,14,128]{3,0,2,1:T(1,128)S(1)} async-done(((f32[1,8,14,128]{3,0,2,1:T(1,128)}), f32[1,8,14,128]{3,0,2,1:T(1,128)S(1)}, u32[]{:S(2)}, u32[]{:S(2)}) %all-to-all-start) | async-done | bytes 57376 | tf_op jit(solution)/shard_map/all_to_all | solution.py:44
  63.6 0.1 multiply_reduce_fusion
  63.8 0.1 fusion.15
  63.9 13.2 %all-gather.1 = bf16[4,2,1792]{2,1,0:T(2,128)(2,1)S(1)} all-gather(bf16[1,2,1792]{2,1,0:T(2,128)(2,1)S(1)} %fusion.15), channel_id=1, replica_groups=mesh['group'=2,'seq'=4,'tensor'=4] {'seq'}, dimensions={0}, use_global_device_ids=true | all-gather | bytes 35840 | tf_op jit(solution)/shard_map/all_gather | solution.py:55
  77.1 6.4 %fusion.20 = f32[8,3584]{1,0:T(8,128)S(1)} fusion(bf16[8,1792]{1,0:T(8,128)(2,1)S(1)} %reshape.152, bf16[1792,3584]{1,0:T(8,128)(2,1)} %param.15), kind=kOutput, calls=%fused_computation.41 | convolution fusion | flops 102760448 | bytes 12988416 | tf_op jit(solution)/shard_map/dot_general | solution.py:57
  83.5 11.3 %all-reduce = bf16[8,3584]{1,0:T(8,128)(2,1)S(1)} all-reduce(f32[8,3584]{1,0:T(8,128)S(1)} %fusion.20), channel_id=2, replica_groups=mesh['group'=2,'seq'=4,'tensor'=4] {'tensor'}, use_global_device_ids=true, to_apply=%region_7.8.clone | all-reduce | flops 28672 | bytes 172032
  94.7 0.6 dynamic-slice_convert_fusion
  (7 shorter events, 0.1 us)
Async XLA Ops:
  0.0 2.1 %copy-start = (s32[8]{0:T(128)S(1)}, s32[8]{0:T(128)}, u32[]{:S(2)}) copy-start(s32[8]{0:T(128)} %param.14) | copy-start | bytes 100
  25.2 2.7 %copy-start.1 = (f32[14]{0:T(128)S(1)}, f32[14]{0:T(128)}, u32[]{:S(2)}) copy-start(f32[14]{0:T(128)} %param.11) | copy-start | bytes 172
  28.8 15.2 %all-to-all-start.1 = ((f32[1,8,14]{2,0,1:T(1,128)}), f32[1,8,14]{2,0,1:T(1,128)S(1)}, u32[]{:S(2)}, u32[]{:S(2)}) async-start(f32[1,8,14]{2,0,1:T(1,128)} %copy.54), calls=%async_computation.1 | async-start | bytes 8192 | tf_op jit(solution)/shard_map/all_to_all | solution.py:42
  39.8 9.9 %copy-start.2 = (u32[32]{0:T(128)S(1)}, u32[32]{0:T(128)}, u32[]{:S(2)}) copy-start(u32[32]{0:T(128)} %constant.39) | copy-start | bytes 388
  44.0 10.7 %all-to-all-start.2 = ((f32[1,8,14]{2,0,1:T(1,128)}), f32[1,8,14]{2,0,1:T(1,128)S(1)}, u32[]{:S(2)}, u32[]{:S(2)}) async-start(f32[1,8,14]{2,0,1:T(1,128)} %copy.57), calls=%async_computation.2 | async-start | bytes 8192 | tf_op jit(solution)/shard_map/all_to_all | solution.py:43
  54.6 9.0 %all-to-all-start = ((f32[1,8,14,128]{3,0,2,1:T(1,128)}), f32[1,8,14,128]{3,0,2,1:T(1,128)S(1)}, u32[]{:S(2)}, u32[]{:S(2)}) async-start(f32[1,8,14,128]{3,0,2,1:T(1,128)} %copy.51), calls=%async_computation | async-start | bytes 114688 | tf_op jit(solution)/shard_map/all_to_all | solution.py:44
where the time goes:
time: 96.1 us; the launch traced here: 95.4 us
  blocking collectives  39.5 us (41%)
  local copies, waits for them, and re-layouts  16.7 us (17%)
  starting transfers between devices  13.1 us (14%)
  matrix products  12.5 us (13%)
  waiting for transfers between devices  9.12 us (9%)
  other arithmetic  3.75 us (4%)
    all_gather x1, blocking collectives, local(): whole_query = lax.all_gather(query, 'seq', axis=0, tiled=True)  15.1 us
    all_gather x1, blocking collectives, local(): attention = lax.all_gather(mine, 'seq', axis=0, tiled=True)  13.2 us
    unnamed x11, local copies, waits for them, and re-layouts  12.6 us
    unnamed x1, blocking collectives  11.3 us
    dot_general x1, matrix products, local(): jnp.dot(attention, out_weight, preferred_element_type=jnp.float32)  6.41 us
    all_to_all x1, waiting for transfers between devices, local(): lax.all_to_all(local_acc[None], 'seq', split_axis=1, concat_axis=0, tiled...  5.46 us
    all_to_all x1, starting transfers between devices, local(): lax.all_to_all(local_total[None], 'seq', split_axis=1, concat_axis=0, til...  5.09 us
    all_to_all x1, starting transfers between devices, local(): lax.all_to_all(local_top[None], 'seq', split_axis=1, concat_axis=0, tiled...  4.74 us
  transfers between devices with their start and end apart: 3, of which 2 were waited for; matrix products, arithmetic and copies ran while one was open for 13% of the time, Pallas kernels for 0%

commit v1 on v0

--- a/solution.py
+++ b/solution.py
@@ -52,7 +52,15 @@
         .astype(jnp.bfloat16)
         .reshape(home_acc.shape[0], features)
     )
-    attention = lax.all_gather(mine, "seq", axis=0, tiled=True)
+    ways, here = (lax.axis_size("seq"), lax.axis_index("seq"))
+    grown, reach = (mine, 1)
+    while reach < ways:
+        theirs = lax.ppermute(grown, "seq", [(d, d ^ reach) for d in range(ways)])
+        mine_first = jnp.concatenate([grown, theirs], axis=0)
+        theirs_first = jnp.concatenate([theirs, grown], axis=0)
+        grown = jnp.where(here & reach == 0, mine_first, theirs_first)
+        reach = 2 * reach
+    attention = grown
     mixed = lax.psum_scatter(
         jnp.dot(attention, out_weight, preferred_element_type=jnp.float32),
         "tensor",

time: 96.1 us -> 90.9 us (0.946)
  blocking collectives: 39.5 us -> 26.3 us
  waiting for transfers between devices: 9.12 us -> 15.3 us
  starting transfers between devices: 13.1 us -> 14.9 us
    all_gather x1 -> x0, blocking collectives: 13.2 us -> none  [local(): attention = lax.all_gather(mine, 'seq', axis=0, tiled=True)]
    ppermute x0 -> x2, waiting for transfers between devices: none -> 5.32 us  [local(): theirs = lax.ppermute(grown, 'seq', [(d, d ^ reach) for d in range(ways)])]
    ppermute x0 -> x2, starting transfers between devices: none -> 1.82 us  [local(): theirs = lax.ppermute(grown, 'seq', [(d, d ^ reach) for d in range(ways)])]
    unnamed x11 -> x10, local copies, waits for them, and re-layouts: 12.6 us -> 12.5 us
  transfers between devices with their start and end apart: 3 -> 5, of which waited for: 2 -> 4; matrix products, arithmetic and copies ran while one was open for 13% -> 13% of each run, Pallas kernels for 0% -> 0%
where the time goes in v1:
time: 90.9 us; the launch traced here: 90.2 us
  blocking collectives  26.3 us (29%)
  local copies, waits for them, and re-layouts  16.6 us (18%)
  waiting for transfers between devices  15.3 us (17%)
  starting transfers between devices  14.9 us (16%)
  matrix products  12.5 us (14%)
  other arithmetic  3.8 us (4%)
    all_gather x1, blocking collectives, local(): whole_query = lax.all_gather(query, 'seq', axis=0, tiled=True)  15.1 us
    unnamed x10, local copies, waits for them, and re-layouts  12.5 us
    unnamed x1, blocking collectives  11.3 us
    dot_general x1, matrix products, local(): jnp.dot(attention, out_weight, preferred_element_type=jnp.float32)  6.4 us
    all_to_all x1, waiting for transfers between devices, local(): lax.all_to_all(local_acc[None], 'seq', split_axis=1, concat_axis=0, tiled...  5.46 us
    ppermute x2, waiting for transfers between devices, local(): theirs = lax.ppermute(grown, 'seq', [(d, d ^ reach) for d in range(ways)])  5.32 us
    all_to_all x1, starting transfers between devices, local(): lax.all_to_all(local_total[None], 'seq', split_axis=1, concat_axis=0, til...  5.09 us
    all_to_all x1, starting transfers between devices, local(): lax.all_to_all(local_top[None], 'seq', split_axis=1, concat_axis=0, tiled...  4.74 us
  transfers between devices with their start and end apart: 5, of which 4 were waited for; matrix products, arithmetic and copies ran while one was open for 13% of the time, Pallas kernels for 0%

profile of v1, /device:TPU:0, one launch (start us, length us, event | category | flops | bytes accessed | tf_op | source)
XLA Modules:
  0.0 90.2 jit_solution(6438257981220577048)
XLA Ops:
  0.0 0.0 copy-start
  0.0 0.7 compare_select_fusion
  0.7 0.7 compare_and_fusion
  1.3 0.7 iota_compare_fusion
  2.1 0.0 copy-done
  2.1 0.6 gather_fusion
  2.7 0.7 broadcast_add_fusion
  3.4 0.1 fusion.23
  3.5 0.1 subtract_convert_fusion
  3.5 15.1 %all-gather = bf16[4,2,1792]{2,1,0:T(2,128)(2,1)S(1)} all-gather(bf16[1,2,1792]{2,1,0:T(2,128)(2,1)} %bitcast.40), channel_id=1, replica_groups=mesh['group'=2,'seq'=4,'tensor'=4] {'seq'}, dimensions={0}, use_global_device_ids=true | all-gather | bytes 35840 | tf_op jit(solution)/shard_map/all_gather | solution.py:16
  18.6 0.6 gather_fusion.1
  19.2 6.0 %copy.49 = bf16[4,256,1792]{1,2,0:T(8,128)(2,1)} copy(bf16[4,256,1792]{2,1,0:T(8,128)(2,1)} %param.9) | data formatting | bytes 7340032 | tf_op args[1]
  25.2 0.0 copy-start.1
  25.2 0.1 select_bitcast_fusion
  25.2 2.6 %fusion.15 = f32[4,14,1,256]{3,2,1,0:T(1,128)S(1)} fusion(bf16[4,256,14,128]{1,3,2,0:T(8,128)(2,1)} %bitcast.32, bf16[4,14,128,1]{2,1,0,3:T(8,128)(2,1)S(1)} %select_bitcast_fusion), kind=kOutput, calls=%fused_computation.23 | convolution fusion | flops 3670016 | bytes 3741696 | tf_op jit(solution)/shard_map/bthd,bhd->bht/dot_general | solution.py:21
  27.9 0.0 copy-done.1
  27.9 0.2 fusion.26
  28.0 0.1 select_reduce_fusion
  28.1 0.7 copy.54
  28.8 4.7 %all-to-all-start.1 = ((f32[1,8,14]{2,0,1:T(1,128)}), f32[1,8,14]{2,0,1:T(1,128)S(1)}, u32[]{:S(2)}, u32[]{:S(2)}) async-start(f32[1,8,14]{2,0,1:T(1,128)} %copy.54), calls=%async_computation.1 | async-start | bytes 8192 | tf_op jit(solution)/shard_map/all_to_all | solution.py:42
  33.6 0.2 fusion.4
  33.7 6.0 %copy.50 = bf16[4,256,1792]{1,2,0:T(8,128)(2,1)} copy(bf16[4,256,1792]{2,1,0:T(8,128)(2,1)} %param.10) | data formatting | bytes 7340032 | tf_op args[2]
  39.7 0.0 copy-start.2
  39.7 3.1 %fusion.2 = f32[4,14,1,128]{3,2,1,0:T(1,128)S(1)} fusion(bf16[4,256,14,128]{1,3,2,0:T(8,128)(2,1)} %bitcast.33, bf16[4,14,256,1]{2,0,1,3:T(4,128)(2,1)S(1)} %get-tuple-element.10), kind=kOutput, calls=%fused_computation.6 | convolution fusion | flops 3670016 | bytes 3727360 | tf_op jit(solution)/shard_map/bht,bthd->bhd/dot_general | solution.py:32
  42.8 0.1 multiply_reduce_fusion.1
  42.9 0.7 copy.57
  43.6 0.0 all-to-all-done.1
  43.6 5.1 %all-to-all-start.2 = ((f32[1,8,14]{2,0,1:T(1,128)}), f32[1,8,14]{2,0,1:T(1,128)S(1)}, u32[]{:S(2)}, u32[]{:S(2)}) async-start(f32[1,8,14]{2,0,1:T(1,128)} %copy.57), calls=%async_computation.2 | async-start | bytes 8192 | tf_op jit(solution)/shard_map/all_to_all | solution.py:43
  48.7 0.4 convolution_bitcast_fusion
  49.1 0.7 copy.51
  49.8 4.5 %all-to-all-done.2 = f32[1,8,14]{2,0,1:T(1,128)S(1)} async-done(((f32[1,8,14]{2,0,1:T(1,128)}), f32[1,8,14]{2,0,1:T(1,128)S(1)}, u32[]{:S(2)}, u32[]{:S(2)}) %all-to-all-start.2) | async-done | bytes 480 | tf_op jit(solution)/shard_map/all_to_all | solution.py:43
  54.3 3.3 %all-to-all-start = ((f32[1,8,14,128]{3,0,2,1:T(1,128)}), f32[1,8,14,128]{3,0,2,1:T(1,128)S(1)}, u32[]{:S(2)}, u32[]{:S(2)}) async-start(f32[1,8,14,128]{3,0,2,1:T(1,128)} %copy.51), calls=%async_computation | async-start | bytes 114688 | tf_op jit(solution)/shard_map/all_to_all | solution.py:44
  57.6 0.1 copy.55
  57.7 0.1 copy.58
  57.8 5.5 %all-to-all-done = f32[1,8,14,128]{3,0,2,1:T(1,128)S(1)} async-done(((f32[1,8,14,128]{3,0,2,1:T(1,128)}), f32[1,8,14,128]{3,0,2,1:T(1,128)S(1)}, u32[]{:S(2)}, u32[]{:S(2)}) %all-to-all-start) | async-done | bytes 57376 | tf_op jit(solution)/shard_map/all_to_all | solution.py:44
  63.2 0.1 multiply_reduce_fusion
  63.4 0.1 fusion.22
  63.5 1.0 %collective-permute-start = (bf16[2,1792]{1,0:T(2,128)(2,1)S(1)}, bf16[2,1792]{1,0:T(2,128)(2,1)S(1)}, u32[]{:S(2)}, u32[]{:S(2)}) collective-permute-start(bf16[2,1792]{1,0:T(2,128)(2,1)S(1)} %fusion.22), channel_id=1, source_target_pairs={{0,4},{4,0},{8,12},{12,8},{1,5},{5,1},{9,13},{13,9},{2,6},{6,2},{1... | collective-permute-start | bytes 21512 | tf_op jit(solution)/shard_map/ppermute | solution.py:58
  64.5 2.7 %collective-permute-done = bf16[2,1792]{1,0:T(2,128)(2,1)S(1)} collective-permute-done((bf16[2,1792]{1,0:T(2,128)(2,1)S(1)}, bf16[2,1792]{1,0:T(2,128)(2,1)S(1)}, u32[]{:S(2)}, u32[]{:S(2)}) %collective-permute-start) | collective-permute-done | bytes 7200 | tf_op jit(solution)/shard_map/ppermute | solution.py:58
  67.2 0.8 collective-permute-start.1
  68.0 0.0 copy-done.2
  68.0 0.6 dynamic-slice
  69.2 2.7 %collective-permute-done.1 = bf16[4,1792]{1,0:T(4,128)(2,1)S(1)} collective-permute-done((bf16[4,1792]{1,0:T(4,128)(2,1)S(1)}, bf16[4,1792]{1,0:T(4,128)(2,1)S(1)}, u32[]{:S(2)}, u32[]{:S(2)}) %collective-permute-start.1) | collective-permute-done | bytes 14368 | tf_op jit(solution)/shard_map/ppermute | solution.py:58
  71.9 6.4 %fusion.7 = f32[8,3584]{1,0:T(8,128)S(1)} fusion(bf16[1792,3584]{1,0:T(8,128)(2,1)} %param.15, bf16[4,1792]{1,0:T(4,128)(2,1)S(1)} %collective-permute-done.1, bf16[4,1792]{1,0:T(4,128)(2,1)S(1)} %maximum_select_fusion.2, pred[]{:T(512)S(6)} %eq.23), kind=kOutput, calls=%fused_computation.14 | convolution fusion | flops 102889472 | bytes 12988417 | tf_op jit(solution)/shard_map/dot_general | solution.py:65
  78.3 11.3 %all-reduce = bf16[8,3584]{1,0:T(8,128)(2,1)S(1)} all-reduce(f32[8,3584]{1,0:T(8,128)S(1)} %fusion.7), channel_id=2, replica_groups=mesh['group'=2,'seq'=4,'tensor'=4] {'tensor'}, use_global_device_ids=true, to_apply=%region_7.8.clone | all-reduce | flops 28672 | bytes 172032
  89.6 0.6 dynamic-slice_convert_fusion
  (7 shorter events, 0.1 us)
Async XLA Ops:
  0.0 2.1 %copy-start = (s32[8]{0:T(128)S(1)}, s32[8]{0:T(128)}, u32[]{:S(2)}) copy-start(s32[8]{0:T(128)} %param.14) | copy-start | bytes 100
  25.2 2.7 %copy-start.1 = (f32[14]{0:T(128)S(1)}, f32[14]{0:T(128)}, u32[]{:S(2)}) copy-start(f32[14]{0:T(128)} %param.11) | copy-start | bytes 172
  28.8 14.8 %all-to-all-start.1 = ((f32[1,8,14]{2,0,1:T(1,128)}), f32[1,8,14]{2,0,1:T(1,128)S(1)}, u32[]{:S(2)}, u32[]{:S(2)}) async-start(f32[1,8,14]{2,0,1:T(1,128)} %copy.54), calls=%async_computation.1 | async-start | bytes 8192 | tf_op jit(solution)/shard_map/all_to_all | solution.py:42
  39.7 28.3 %copy-start.2 = (u32[32]{0:T(128)S(1)}, u32[32]{0:T(128)}, u32[]{:S(2)}) copy-start(u32[32]{0:T(128)} %constant.49) | copy-start | bytes 388
  43.6 10.7 %all-to-all-start.2 = ((f32[1,8,14]{2,0,1:T(1,128)}), f32[1,8,14]{2,0,1:T(1,128)S(1)}, u32[]{:S(2)}, u32[]{:S(2)}) async-start(f32[1,8,14]{2,0,1:T(1,128)} %copy.57), calls=%async_computation.2 | async-start | bytes 8192 | tf_op jit(solution)/shard_map/all_to_all | solution.py:43
  54.3 9.0 %all-to-all-start = ((f32[1,8,14,128]{3,0,2,1:T(1,128)}), f32[1,8,14,128]{3,0,2,1:T(1,128)S(1)}, u32[]{:S(2)}, u32[]{:S(2)}) async-start(f32[1,8,14,128]{3,0,2,1:T(1,128)} %copy.51), calls=%async_computation | async-start | bytes 114688 | tf_op jit(solution)/shard_map/all_to_all | solution.py:44
  63.5 3.7 %collective-permute-start = (bf16[2,1792]{1,0:T(2,128)(2,1)S(1)}, bf16[2,1792]{1,0:T(2,128)(2,1)S(1)}, u32[]{:S(2)}, u32[]{:S(2)}) collective-permute-start(bf16[2,1792]{1,0:T(2,128)(2,1)S(1)} %fusion.22), channel_id=1, source_target_pairs={{0,4},{4,0},{8,12},{12,8},{1,5},{5,1},{9,13},{13,9},{2,6},{6,2},{1... | collective-permute-start | bytes 21512 | tf_op jit(solution)/shard_map/ppermute | solution.py:58
  67.2 4.7 %collective-permute-start.1 = (bf16[4,1792]{1,0:T(4,128)(2,1)S(1)}, bf16[4,1792]{1,0:T(4,128)(2,1)S(1)}, u32[]{:S(2)}, u32[]{:S(2)}) collective-permute-start(bf16[4,1792]{1,0:T(4,128)(2,1)S(1)} %maximum_select_fusion.2), channel_id=1, source_target_pairs={{0,8},{4,12},{8,0},{12,4},{1,9},{5,13},{9,1},{13,5},{2,10},{6,14},... | collective-permute-start | bytes 43016 | tf_op jit(solution)/shard_map/ppermute | solution.py:58
